TPU v7x, 256 devices: a whole 4x4x8 slice. The times are simulated.
256 devices in a mesh: dp: 32 (over x, y, core), adapter: 8 (over z).
Axes of the slice: x: 4, y: 4, z: 8, core: 2. Of those that a mesh axis runs over, the one named last changes fastest.
Arguments:
- tokens: bfloat16 [32768, 1024], P('dp'), may hold values from -60 to 60
- down_weight: bfloat16 [16, 1024, 64], P('adapter'), may hold values from -0.1875 to 0.1875
- down_bias: bfloat16 [16, 64], P('adapter'), may hold values from -3 to 3
- up_weight: bfloat16 [16, 64, 1024], P('adapter'), may hold values from -0.75 to 0.75
- up_bias: bfloat16 [16, 1024], P('adapter'), may hold values from -3 to 3
- query_weight: bfloat16 [1024, 1024], P(('dp', 'adapter')), may hold values from -0.1875 to 0.1875
- key_weight: bfloat16 [1024, 1024], P(('dp', 'adapter')), may hold values from -0.1875 to 0.1875
- value_weight: bfloat16 [1024, 1024], P(('dp', 'adapter')), may hold values from -0.1875 to 0.1875
Outputs:
- united_out: bfloat16 [32768, 1024], P(('dp', 'adapter'))
All inputs are finite; a program needn't handle non-finite values.
Results may differ from a plain program's by a relative error of at most 0.012.
The roundings to bfloat16 on the way count: a program that leaves them out, or rounds other values in their place, can miss the bound.
Values may be sent and summed in bfloat16 or wider, within the bound.
A program may use at most 64 MiB of HBM per device.

v0:
```python
import math

import jax
import jax.numpy as jnp
from jax import lax
from jax.sharding import PartitionSpec as P


def in_one_piece(arrays, axis, dim, along):
    widths = [a.shape[along] for a in arrays]
    both = jnp.concatenate(arrays, axis=along)
    filled = lax.all_gather(both, axis, axis=dim, tiled=True)
    return tuple(jnp.split(filled, [sum(widths[:k]) for k in range(1, len(widths))], axis=along))


def from_everyone(value, axis):
    copies = jnp.broadcast_to(value, (lax.axis_size(axis), *value.shape))
    return lax.all_to_all(copies, axis, split_axis=0, concat_axis=0, tiled=True)


def taken_together(value, axis):
    everything = from_everyone(value, axis)
    return jnp.max(everything, axis=0)


def taken_together_2(value, axis):
    return from_everyone(value, axis).sum(axis=0)


def adapt_rows(rows, down_weight, down_bias, up_weight, up_bias):
    rows_float = rows.astype(jnp.float32)
    hidden = jnp.einsum("td,adr->atr", rows, down_weight, preferred_element_type=jnp.float32)
    hidden = jax.nn.relu(hidden + down_bias.astype(jnp.float32)[:, None, :]).astype(jnp.bfloat16)
    lifted = jnp.einsum("atr,ard->atd", hidden, up_weight, preferred_element_type=jnp.float32)
    return (rows_float[None] + lifted + up_bias.astype(jnp.float32)[:, None, :]).astype(
        jnp.bfloat16
    )


def body(
    tokens, down_weight, down_bias, up_weight, up_bias, query_weight, key_weight, value_weight
):
    tok_rows, feature_width = tokens.shape
    score_scale = 1.0 / math.sqrt(feature_width)
    tok_float = tokens.astype(jnp.float32)
    block_q, block_k, block_v = in_one_piece(
        (query_weight, key_weight, value_weight), "adapter", 0, 1
    )
    whole_q, whole_k, whole_v = in_one_piece((block_q, block_k, block_v), "dp", 0, 1)
    share = tok_rows // lax.axis_size("adapter")
    begin = lax.axis_index("adapter") * share
    own_tokens = lax.dynamic_slice_in_dim(tok_float, begin, share, 0)
    adapted = adapt_rows(tokens, down_weight, down_bias, up_weight, up_bias)
    local_count = adapted.shape[0]
    flat = adapted.reshape(local_count * tok_rows, feature_width)
    query_rows = jnp.dot(tokens, whole_q, preferred_element_type=jnp.float32)
    key_rows = jnp.dot(flat, whole_k, preferred_element_type=jnp.float32).reshape(
        local_count, tok_rows, feature_width
    )
    value_rows = jnp.dot(flat, whole_v, preferred_element_type=jnp.float32).reshape(
        local_count, tok_rows, feature_width
    )
    scores = jnp.sum(key_rows * query_rows[None], axis=2) * score_scale
    peak = taken_together(jnp.max(scores, axis=0), "adapter")
    expo = jnp.exp(scores - peak[None])
    denominator = taken_together_2(jnp.sum(expo, axis=0), "adapter")
    local_summed = jnp.sum(expo[:, :, None] * value_rows, axis=0)
    own_summed = lax.psum_scatter(
        local_summed.astype(jnp.bfloat16), "adapter", scatter_dimension=0, tiled=True
    ).astype(jnp.float32)
    united_rows = own_summed / lax.dynamic_slice_in_dim(denominator, begin, share, 0)[:, None]
    return (own_tokens + united_rows).astype(jnp.bfloat16)


def solution(mesh):
    in_specs = (
        P("dp", None),
        P("adapter", None, None),
        P("adapter", None),
        P("adapter", None, None),
        P("adapter", None),
        P(("dp", "adapter"), None),
        P(("dp", "adapter"), None),
        P(("dp", "adapter"), None),
    )
    out_specs = P(("dp", "adapter"), None)
    return jax.shard_map(body, mesh=mesh, in_specs=in_specs, out_specs=out_specs, check_vma=False)
```

profile of v0, /device:TPU:2, one launch (start us, length us, event | category | flops | bytes accessed | tf_op | source)
XLA Modules:
  0.0 171.0 jit_solution(2193434595878431103)
XLA Ops:
  6.5 0.0 copy-start
  6.5 0.0 copy-start.1
  6.5 0.0 copy-start.4
  6.5 0.0 copy-start.5
  6.5 0.0 copy-start.3
  6.5 0.0 all-gather.3.cloned.1.call-start
  6.6 0.9 maximum_bitcast_fusion
  7.5 28.4 %all-gather = bf16[8,4,3072]{2,1,0:T(4,128)(2,1)S(1)} all-gather(bf16[1,4,3072]{2,1,0:T(4,128)(2,1)S(1)} %maximum_bitcast_fusion), channel_id=1, replica_groups=mesh['dp'=32,'adapter'=8] {'adapter'}, dimensions={0}, use_global_device_ids=true | all-gather | bytes 221184 | tf_op jit(solution)/shard_map/all_gather | solution.py:12
  35.9 0.7 reshape.37
  36.6 0.0 all-gather.3.cloned.1.call-update
  36.7 0.0 reduce-scatter.2.cloned.1.call-start
  36.7 4.1 %convert_element_type.26 = f32[1024,1024]{1,0:T(8,128)} convert(bf16[1024,1024]{1,0:T(8,128)(2,1)} %param.8) | non-fusion elementwise | flops 1048576 | bytes 6291456 | tf_op jit(solution)/shard_map/convert_element_type | solution.py:45
  40.8 0.0 copy-done.4
  40.8 0.0 copy-done.5
  40.8 0.0 copy-done
  40.8 0.0 copy-done.1
  40.8 0.0 copy-done.3
  40.9 5.4 %add_convert_fusion = bf16[2,1024,1024]{2,1,0:T(8,128)(2,1)} fusion(f32[2,1024]{1,0:T(2,128)S(1)} %convert_element_type.29, f32[1024,1024]{1,0:T(8,128)} %convert_element_type.26, bf16[2,64,1024]{2,1,0:T(8,128)(2,1)S(1)} %copy-done, bf16[2,1024,64]{1,2,0:T(8,128)(2,1)S(1)} %copy-done.3, bf16[1024,1024]{1,0:T(8,128)(2,1)S(1)} %copy-done.1, ...), kind=kOutput, calls=%fused_computation.2 | convolution fusion | flops 543555584 | bytes 11018752 | tf_op jit(solution)/shard_map/atr,ard->atd/dot_general | solution.py:34
  46.2 42.8 %all-gather.3.cloned.1.call-done = bf16[1024,3072]{1,0:T(8,128)(2,1)} async-done(((bf16[32,3072]{1,0:T(8,128)(2,1)}), bf16[1024,3072]{1,0:T(8,128)(2,1)}) %all-gather.3.cloned.1.call-update) | async-done | bytes 6291472 | tf_op jit(solution)/shard_map/all_gather | solution.py:12
  89.0 0.0 copy-start.2
  89.0 4.1 %convolution_bitcast_fusion = f32[1024,1024]{0,1:T(8,128)S(1)} fusion(bf16[1024,1024]{1,0:T(8,128)(2,1)S(1)} %copy-done.1, bf16[1024,3072]{1,0:T(8,128)(2,1)} %all-gather.3.cloned.1.call-done), kind=kOutput, calls=%fused_computation.3 | convolution fusion | flops 2147483648 | bytes 8388608 | tf_op jit(solution)/shard_map/dot_general | solution.py:56
  93.2 0.0 copy-done.2
  93.2 6.8 %multiply_reduce_fusion.1 = f32[2,1024]{1,0:T(2,128)S(1)} fusion(f32[1024,1024]{0,1:T(8,128)S(1)} %convolution_bitcast_fusion, bf16[2,1024,1024]{2,1,0:T(8,128)(2,1)S(1)} %copy-done.2, bf16[1024,3072]{1,0:T(8,128)(2,1)} %all-gather.3.cloned.1.call-done), kind=kOutput, calls=%fused_computation.1 | convolution fusion | flops 4299159552 | bytes 10493952 | tf_op jit(solution)/shard_map/dot_general | solution.py:57
  100.1 14.8 %all_to_all.12 = f32[8,1,1024]{2,1,0:T(1,128)S(1)} all-to-all(f32[8,1,1024]{2,1,0:T(1,128)S(1)} %broadcast_in_dim.4), channel_id=1, replica_groups=mesh['dp'=32,'adapter'=8] {'adapter'}, dimensions={0} | all-to-all | bytes 65536 | tf_op jit(solution)/shard_map/all_to_all | solution.py:18
  115.0 9.6 %multiply_reduce_fusion = bf16[1024,1024]{1,0:T(8,128)(2,1)} fusion(f32[2,1024]{1,0:T(2,128)S(1)} %get-tuple-element.6, bf16[2,1024,1024]{2,1,0:T(8,128)(2,1)} %add_convert_fusion, bf16[1024,3072]{1,0:T(8,128)(2,1)} %all-gather.3.cloned.1.call-done), kind=kOutput, calls=%fused_computation | convolution fusion | flops 4298113024 | bytes 8396800 | tf_op jit(solution)/shard_map/dot_general | solution.py:60
  124.5 0.0 reduce-scatter.2.cloned.1.call-update
  124.5 0.6 broadcast_in_dim.5
  125.2 3.3 %all-to-all-start.1 = ((f32[8,1,1024]{2,1,0:T(1,128)}), f32[8,1,1024]{2,1,0:T(1,128)S(1)}, u32[]{:S(2)}, u32[]{:S(2)}) async-start(f32[8,1,1024]{2,1,0:T(1,128)} %broadcast_in_dim.5), calls=%async_computation.2 | async-start | bytes 65536 | tf_op jit(solution)/shard_map/all_to_all | solution.py:18
  128.5 8.0 %all-to-all-done.1 = f32[8,1,1024]{2,1,0:T(1,128)S(1)} async-done(((f32[8,1,1024]{2,1,0:T(1,128)}), f32[8,1,1024]{2,1,0:T(1,128)S(1)}, u32[]{:S(2)}, u32[]{:S(2)}) %all-to-all-start.1) | async-done | bytes 32800 | tf_op jit(solution)/shard_map/all_to_all | solution.py:18
  136.6 0.1 dynamic_slice.7
  136.7 25.5 %reduce-scatter.2.cloned.1.call-done = bf16[128,1024]{1,0:T(8,128)(2,1)} async-done(((bf16[1024,1024]{1,0:T(8,128)(2,1)}), bf16[128,1024]{1,0:T(8,128)(2,1)}) %reduce-scatter.2.cloned.1.call-update) | async-done | bytes 262160 | tf_op jit(solution)/shard_map/reduce_scatter | solution.py:68
  162.2 2.0 %add_convert_fusion.1 = bf16[128,1024]{1,0:T(8,128)(2,1)} fusion(bf16[128,1024]{1,0:T(8,128)(2,1)} %reduce-scatter.2.cloned.1.call-done, f32[1024,1024]{1,0:T(8,128)} %convert_element_type.26, s32[]{:T(128)S(6)} %select_n.4, f32[128]{0:T(128)S(1)} %dynamic_slice.7), kind=kLoop, calls=%fused_computation.12 | loop fusion | flops 524288 | bytes 1049092 | tf_op jit(solution)/shard_map/convert_element_type | solution.py:72
  (7 shorter events, 0.1 us)
Async XLA Ops:
  6.5 34.3 %copy-start = (bf16[2,64,1024]{2,1,0:T(8,128)(2,1)S(1)}, bf16[2,64,1024]{2,1,0:T(8,128)(2,1)}, u32[]{:S(2)}) copy-start(bf16[2,64,1024]{2,1,0:T(8,128)(2,1)} %param.11) | copy-start | bytes 786436
  6.5 34.3 %copy-start.1 = (bf16[1024,1024]{1,0:T(8,128)(2,1)S(1)}, bf16[1024,1024]{1,0:T(8,128)(2,1)}, u32[]{:S(2)}) copy-start(bf16[1024,1024]{1,0:T(8,128)(2,1)} %param.8) | copy-start | bytes 6291460
  6.5 34.3 %copy-start.4 = (bf16[2,1024]{1,0:T(2,128)(2,1)S(1)}, bf16[2,1024]{1,0:T(2,128)(2,1)}, u32[]{:S(2)}) copy-start(bf16[2,1024]{1,0:T(2,128)(2,1)} %param.12) | copy-start | bytes 12292
  6.5 34.3 %copy-start.5 = (bf16[2,64]{1,0:T(2,128)(2,1)S(1)}, bf16[2,64]{1,0:T(2,128)(2,1)}, u32[]{:S(2)}) copy-start(bf16[2,64]{1,0:T(2,128)(2,1)} %param.10) | copy-start | bytes 772
  6.5 34.3 %copy-start.3 = (bf16[2,1024,64]{1,2,0:T(8,128)(2,1)S(1)}, bf16[2,1024,64]{1,2,0:T(8,128)(2,1)}, u32[]{:S(2)}) copy-start(bf16[2,1024,64]{1,2,0:T(8,128)(2,1)} %param.9) | copy-start | bytes 786436
  6.5 82.5 %all-gather.3.cloned.1.call-start = ((), (), s32[]{:S(2)}) async-start(), calls=%async_computation.3 | async-start | bytes 6488064 | tf_op jit(solution)/shard_map/all_gather | solution.py:12
  36.7 125.5 %reduce-scatter.2.cloned.1.call-start = ((), (), s32[]{:S(2)}) async-start(), calls=%async_computation.4 | async-start | bytes 2359296 | tf_op jit(solution)/shard_map/reduce_scatter | solution.py:68
  89.0 4.1 %copy-start.2 = (bf16[2,1024,1024]{2,1,0:T(8,128)(2,1)S(1)}, bf16[2,1024,1024]{2,1,0:T(8,128)(2,1)}, u32[]{:S(2)}) copy-start(bf16[2,1024,1024]{2,1,0:T(8,128)(2,1)} %add_convert_fusion) | copy-start | bytes 12582916
  125.2 11.4 %all-to-all-start.1 = ((f32[8,1,1024]{2,1,0:T(1,128)}), f32[8,1,1024]{2,1,0:T(1,128)S(1)}, u32[]{:S(2)}, u32[]{:S(2)}) async-start(f32[8,1,1024]{2,1,0:T(1,128)} %broadcast_in_dim.5), calls=%async_computation.2 | async-start | bytes 65536 | tf_op jit(solution)/shard_map/all_to_all | solution.py:18
Sparse Core Ops, SparseCore 0:
  36.8 52.2 all-gather.2
  124.7 37.4 reduce-scatter.1
where the time goes:
time: 171 us
  waiting for transfers between devices  76.3 us (45%)
  blocking collectives  43.2 us (25%)
  matrix products  25.9 us (15%)
  between operations  13.5 us (8%)
  other arithmetic  7.06 us (4%)
  starting transfers between devices  3.42 us (2%)
    all_gather x1, waiting for transfers between devices, in_one_piece(): filled = lax.all_gather(both, axis, axis=dim, tiled=True)  42.8 us
    all_gather x1, blocking collectives, in_one_piece(): filled = lax.all_gather(both, axis, axis=dim, tiled=True)  28.4 us
    reduce_scatter x1, waiting for transfers between devices, body(): lax.psum_scatter(local_summed.astype(jnp.bfloat16), 'adapter', scatter_di...  25.5 us
    all_to_all x1, blocking collectives, from_everyone(): return lax.all_to_all(copies, axis, split_axis=0, concat_axis=0, tiled=True)  14.8 us
    dot_general x1, matrix products, body(): jnp.dot(flat, whole_v, preferred_element_type=jnp.float32)  9.55 us
    all_to_all x1, waiting for transfers between devices, from_everyone(): return lax.all_to_all(copies, axis, split_axis=0, concat_axis=0, tiled=True)  8.04 us
    dot_general x1, matrix products, body(): jnp.dot(flat, whole_k, preferred_element_type=jnp.float32)  6.83 us
    dot_general x1, matrix products, adapt_rows(): jnp.einsum('atr,ard->atd', hidden, up_weight, preferred_element_type=jnp....  5.38 us
  transfers between devices with their start and end apart: 3, of which 3 were waited for; matrix products, arithmetic and copies ran while one was open for 6% of the time, Pallas kernels for 0%

commit v1 on v0

v1 whole, which is shorter than its diff:
```python
import functools

import jax
import jax.numpy as jnp
from jax import lax
from jax.experimental import pallas as pl
from jax.experimental.pallas import tpu as pltpu
from jax.sharding import PartitionSpec as P

BF16, F32 = jnp.bfloat16, jnp.float32
NX, NY, NC, NZ = 4, 4, 2, 8
Z_STEPS = (4, 3, -3, 2, -2, 1, -1)
NT = (((1,), (1,)), ((), ()))


class Copy:
    def __init__(self, name, region, step, needs, size, front=0.0):
        self.name, self.region, self.step = name, region, step
        self.needs, self.size, self.front = needs, size, front


class Work:
    def __init__(self, name, run, needs, cost):
        self.name, self.run, self.needs, self.cost = name, run, needs, cost


def plan_copies():
    copies = {}

    def add(name, region, step, needs, size, front=0.0):
        copies[name] = Copy(name, region, step, tuple(needs), size, front)

    def page(m):
        return lambda r, x, y, c, z: r["w"].at[m, x, y, c, pl.ds(4 * z, 4)]

    for m in range(3):
        for d in Z_STEPS:
            add(("page", m, d), page(m), (0, 0, 0, d), (), 8)
    for d in Z_STEPS:
        add(("ub", d), lambda r, x, y, c, z: r["ub"].at[z], (0, 0, 0, d), (), 4)
        add(("db", d), lambda r, x, y, c, z: r["db"].at[z], (0, 0, 0, d), (), 1)

    def ring(buf, back):
        return lambda r, x, y, c, z: r[buf].at[(z + back + NZ) % NZ, c]

    for s in range(1, 5):
        for buf, way in (("dn", 1), ("up", -1), ("up", 1), ("dn", -1)):
            if s == 4 and (buf, way) in (("up", 1), ("dn", -1)):
                continue
            needs = [("ring", buf, way, s - 1)] if s > 1 else []
            add(("ring", buf, way, s), ring(buf, -way * (s - 1)), (0, 0, 0, way), needs, 128)
    for buf in ("dn", "up"):
        for k in (-1, 1, -2, 2, -3, 3, 4):
            src = ("ring", buf, 1, -k) if k < 0 else ("ring", buf, -1, k)
            if k == 4 and buf == "dn":
                src = ("ring", "dn", 1, 4)
            add(("pair", buf, k), ring(buf, k), (0, 0, 1, 0), [src], 128)

    def block(m, h, i, j, lo, rows):
        def at(r, x, y, c, z):
            a, b = (x, y) if h == 0 else (y, x)
            a, b = (a + i + 4) % 4, (b + j + 4) % 4
            x, y = (a, b) if h == 0 else (b, a)
            return r["w"].at[m, x, y, c, pl.ds(16 * h + lo, rows)]

        return at

    def line(m, h, j, lo, rows):
        def at(r, x, y, c, z):
            if h == 0:
                return r["w"].at[m, :, (y + j + 4) % 4, c, pl.ds(16 * h + lo, rows)]
            return r["w"].at[m, (x + j + 4) % 4, :, c, pl.ds(16 * h + lo, rows)]

        return at

    for m in range(3):
        mine = [("page", m, d) for d in Z_STEPS]
        for h in range(2):
            along = (lambda d: (d, 0, 0, 0)) if h == 0 else (lambda d: (0, d, 0, 0))
            across = (lambda d: (0, d, 0, 0)) if h == 0 else (lambda d: (d, 0, 0, 0))
            key = (m, h)
            for d in (1, -1):
                add(("s1", key, d), block(m, h, 0, 0, 0, 16), along(d), mine, 32)
                add(("s3", key, 0, d), block(m, h, 0, 0, 0, 16), across(d), mine, 32)
            for d in (1, -1):
                lo = 0 if d == 1 else 8
                add(("s2", key, d), block(m, h, -d, 0, lo, 8), along(d), [("s1", key, d)], 16)
            for i in (-1, 1, 2):
                src = [("s1", key, -i)] if i != 2 else [("s2", key, 1), ("s2", key, -1)]
                for d in (1, -1):
                    add(("s3", key, i, d), block(m, h, i, 0, 0, 16), across(d), src, 32)
            for d in (1, -1):
                lo = 0 if d == 1 else 8
                got = [("s3", key, i, d) for i in (0, -1, 1, 2)]
                add(("s4", key, d), line(m, h, -d, lo, 8), across(d), got, 64)
            add(
                ("hand", key, 0),
                line(m, h, 0, 0, 16),
                (0, 0, 1, 0),
                mine + [("s1", key, 1), ("s1", key, -1), ("s2", key, 1), ("s2", key, -1)],
                128,
            )
            for d in (1, -1):
                got = [("s3", key, i, d) for i in (0, -1, 1, 2)]
                add(("hand", key, -d), line(m, h, -d, 0, 16), (0, 0, 1, 0), got, 128)
            add(("hand", key, 2), line(m, h, 2, 0, 16), (0, 0, 1, 0), [("s4", key, 1), ("s4", key, -1)], 128)
    return copies


def all_of(m):
    names = [("page", m, d) for d in Z_STEPS]
    for h in range(2):
        key = (m, h)
        names += [("s1", key, d) for d in (1, -1)] + [("s2", key, d) for d in (1, -1)]
        names += [("s3", key, i, d) for i in (0, -1, 1, 2) for d in (1, -1)]
        names += [("s4", key, d) for d in (1, -1)]
        names += [("hand", key, j) for j in (0, 1, -1, 2)]
    return names


def pair_needs(k):
    if k == 0:
        return []
    d = -k if k != 4 else 4
    names = [("ub", d), ("db", d), ("pair", "dn", k), ("pair", "up", k)]
    for buf in ("dn", "up"):
        src = ("ring", buf, 1, -k) if k < 0 else ("ring", buf, -1, k)
        if k == 4 and buf == "dn":
            src = ("ring", "dn", 1, 4)
        names.append(src)
    return names


def plan_order(copies, works):
    free, arrival, order = {}, {}, []
    now, waited, done = 0.0, set(), set()
    unsent, todo = list(copies), list(works)
    while True:
        moved = True
        while moved:
            moved = False
            for name in list(unsent):
                c = copies[name]
                if all(n in waited for n in c.needs):
                    axis = next(i for i in range(4) if c.step[i])
                    hops = abs(c.step[axis])
                    if axis == 2:
                        link, rate, late = "core", 620.0, 0.9
                    else:
                        link, rate, late = (axis, c.step[axis] > 0), 45.0, 0.95 + 0.8 * hops
                    begin = max(now, free.get(link, 0.0))
                    took = c.size * 1.024 / rate * hops
                    free[link] = begin + took
                    arrival[name] = begin + took + late
                    order.append(("start", name))
                    unsent.remove(name)
                    now += 0.01
                    moved = True
        ready = sorted((t, i, n) for i, (n, t) in enumerate(arrival.items()) if n not in waited)
        if ready and ready[0][0] <= now:
            order.append(("wait", ready[0][2]))
            waited.add(ready[0][2])
            continue
        run = next((w for w in todo if all(n in waited or n in done for n in w.needs)), None)
        if run is not None:
            order.append(("work", run.name))
            now += run.cost
            done.add(run.name)
            todo.remove(run)
            continue
        if not ready:
            break
        now = ready[0][0]
    assert not unsent and not todo
    return order, now


def kernel(
    copies, tokens, dn_in, db_in, up_in, ub_in, q_in, k_in, v_in, out, xs, w, dn, up, db, ub, ad, qhl, qk, mix, loc, ss, rs
):
    dp, z = lax.axis_index("dp"), lax.axis_index("adapter")
    x, y, c = dp // 8, (dp // 2) % 4, dp % 2
    refs = {"w": w, "dn": dn, "up": up, "db": db, "ub": ub}
    ids = {name: i for i, name in enumerate(copies)}

    own = [
        (q_in, w.at[0, x, y, c, pl.ds(4 * z, 4)]),
        (k_in, w.at[1, x, y, c, pl.ds(4 * z, 4)]),
        (v_in, w.at[2, x, y, c, pl.ds(4 * z, 4)]),
        (ub_in, ub.at[z]),
        (db_in, db.at[z]),
        (dn_in, dn.at[z]),
        (up_in, up.at[z]),
        (tokens.at[pl.ds(128 * z, 128)], xs),
    ]
    own = [pltpu.make_async_copy(a, b, loc.at[i]) for i, (a, b) in enumerate(own)]
    for cp in own:
        cp.start()

    def there(step, sign):
        px, py, pz = (x + sign * step[0] + 4) % 4, (y + sign * step[1] + 4) % 4, (z + sign * step[3] + NZ) % NZ
        pc = 1 - c if step[2] else c
        return px, py, pc, pz

    def device(step):
        px, py, pc, pz = there(step, 1)
        return ((px * NY + py) * NC + pc, pz)

    def descriptor(name, sender):
        cp = copies[name]
        region = cp.region(refs, *sender)
        i = ids[name]
        return pltpu.make_async_remote_copy(
            src_ref=region,
            dst_ref=region,
            send_sem=ss.at[i],
            recv_sem=rs.at[i],
            device_id=device(cp.step),
            device_id_type=pl.DeviceIdType.MESH,
        )

    peers = [(0, 0, 0, d) for d in Z_STEPS] + [(1, 0, 0, 0), (-1, 0, 0, 0), (0, 1, 0, 0), (0, -1, 0, 0), (0, 0, 1, 0)]
    barrier = pltpu.get_barrier_semaphore()
    for step in peers:
        pl.semaphore_signal(barrier, inc=1, device_id=device(step), device_id_type=pl.DeviceIdType.MESH)
    pl.semaphore_wait(barrier, len(peers))
    for cp in own:
        cp.wait()

    def adapters(k):
        def run():
            at = (z + k + NZ) % NZ
            bias = db[at].astype(F32)
            bias = jnp.concatenate([bias[0:1], bias[1:2]], axis=1)
            hid = lax.dot_general(xs[...], dn[at].reshape(128, 1024), NT, preferred_element_type=F32)
            hid = jnp.maximum(hid + bias, 0.0).astype(BF16)
            lift = ub[at].astype(F32)
            for i in range(2):
                for n in range(4):
                    cols = slice(256 * n, 256 * n + 256)
                    raised = jnp.dot(hid[:, 64 * i : 64 * i + 64], up[at, i, :, cols], preferred_element_type=F32)
                    ad[2 * ((k + NZ) % NZ) + i, :, cols] = (
                        xs[:, cols].astype(F32) + raised + lift[i : i + 1, cols]
                    ).astype(BF16)

        return run

    def split(part, rows, cols, value):
        high = value.astype(BF16)
        part[rows, cols] = high
        low = slice(rows.start + 128, rows.stop + 128) if isinstance(rows, slice) else rows
        part[low, cols] = (value - high.astype(F32)).astype(BF16)

    def query():
        whole = w.at[0].reshape(1024, 1024)
        for n in range(4):
            cols = slice(256 * n, 256 * n + 256)
            split(qhl, slice(0, 128), cols, jnp.dot(xs[...], whole[:, cols], preferred_element_type=F32))

    def key():
        whole = w.at[1].reshape(1024, 1024)
        for n in range(4):
            cols = slice(256 * n, 256 * n + 256)
            both = lax.dot_general(qhl[...], whole[cols, :], NT, preferred_element_type=F32)
            qk[:, cols] = (both[:128] + both[128:]) * (1.0 / 32.0)

    def attend():
        @pl.loop(0, 8)
        def _(step):
            rows = pl.ds(pl.multiple_of(step * 16, 16), 16)
            weight = qk[rows, :]
            scores = [jnp.sum(ad[a, rows, :].astype(F32) * weight, axis=1, keepdims=True) for a in range(16)]
            peak = functools.reduce(jnp.maximum, scores)
            scores = [jnp.exp(s - peak) for s in scores]
            scale = 1.0 / functools.reduce(jnp.add, scores)
            total = scores[0] * ad[0, rows, :].astype(F32)
            for a in range(1, 16):
                total = total + scores[a] * ad[a, rows, :].astype(F32)
            total = total * scale
            high = total.astype(BF16)
            mix[rows, :] = high
            mix[pl.ds(pl.multiple_of(step * 16 + 128, 16), 16), :] = (total - high.astype(F32)).astype(BF16)

    def value():
        whole = w.at[2].reshape(1024, 1024)
        for n in range(4):
            cols = slice(256 * n, 256 * n + 256)
            both = jnp.dot(mix[...], whole[:, cols], preferred_element_type=F32)
            out[:, cols] = (xs[:, cols].astype(F32) + both[:128] + both[128:]).astype(BF16)

    works = [
        Work("q", query, all_of(0), 0.6),
        Work("k", key, ["q"] + all_of(1), 0.8),
    ]
    pairs = [0, -1, 1, -2, 2, -3, 3, 4]
    works += [Work(("a", k), adapters(k), pair_needs(k), 0.6) for k in pairs]
    works.append(Work("s", attend, ["k"] + [("a", k) for k in pairs], 3.0))
    works.append(Work("v", value, ["s"] + all_of(2), 0.8))
    by_name = {job.name: job for job in works}
    order, _ = plan_order(copies, works)
    for kind, name in order:
        if kind == "start":
            descriptor(name, (x, y, c, z)).start()
        elif kind == "wait":
            descriptor(name, there(copies[name].step, -1)).wait_recv()
        else:
            by_name[name].run()
    for name in copies:
        descriptor(name, (x, y, c, z)).wait_send()


def body(tokens, down_weight, down_bias, up_weight, up_bias, query_weight, key_weight, value_weight):
    copies = plan_copies()
    hbm = pl.BlockSpec(memory_space=pl.ANY)
    return pl.pallas_call(
        functools.partial(kernel, copies),
        out_shape=jax.ShapeDtypeStruct((128, 1024), BF16),
        in_specs=[hbm] * 8,
        out_specs=pl.BlockSpec(memory_space=pltpu.VMEM),
        scratch_shapes=[
            pltpu.VMEM((128, 1024), BF16),
            pltpu.VMEM((3, NX, NY, NC, 32, 1024), BF16),
            pltpu.VMEM((NZ, 2, 64, 1024), BF16),
            pltpu.VMEM((NZ, 2, 64, 1024), BF16),
            pltpu.VMEM((NZ, 2, 64), BF16),
            pltpu.VMEM((NZ, 2, 1024), BF16),
            pltpu.VMEM((16, 128, 1024), BF16),
            pltpu.VMEM((256, 1024), BF16),
            pltpu.VMEM((128, 1024), F32),
            pltpu.VMEM((256, 1024), BF16),
            pltpu.SemaphoreType.DMA((8,)),
            pltpu.SemaphoreType.DMA((len(copies),)),
            pltpu.SemaphoreType.DMA((len(copies),)),
        ],
        compiler_params=pltpu.CompilerParams(
            collective_id=0, has_side_effects=True, vmem_limit_bytes=48 * 1024 * 1024
        ),
    )(
        tokens,
        jnp.swapaxes(down_weight, 1, 2),
        down_bias,
        up_weight,
        up_bias,
        query_weight,
        key_weight,
        value_weight,
    )


def solution(mesh):
    in_specs = (
        P("dp", None),
        P("adapter", None, None),
        P("adapter", None),
        P("adapter", None, None),
        P("adapter", None),
        P(("dp", "adapter"), None),
        P(("dp", "adapter"), None),
        P(("dp", "adapter"), None),
    )
    out_specs = P(("dp", "adapter"), None)
    return jax.shard_map(body, mesh=mesh, in_specs=in_specs, out_specs=out_specs, check_vma=False)
```

time: 171 us -> 58.1 us (0.34)
  the two profiles are of different devices: /device:TPU:2 before, /device:TPU:1 now
where the time goes in v1:
time: 58.1 us; the launch traced here: 57.8 us
  Pallas kernels  50.1 us (86%)
  local copies, waits for them, and re-layouts  7.62 us (13%)
    pallas_call x1, Pallas kernels, body(): pl.pallas_call(functools.partial(kernel, copies), out_shape=jax.ShapeDtyp...  50.1 us
    unnamed x17, local copies, waits for them, and re-layouts  7.62 us

profile of v1, /device:TPU:1, one launch (start us, length us, event | category | flops | bytes accessed | tf_op | source)
XLA Modules:
  0.0 57.8 jit_solution(13069009785719897344)
XLA Ops:
  0.0 0.0 copy-start
  0.0 1.6 %copy-done = bf16[1024,1024]{1,0:T(8,128)(2,1)S(1)} copy-done((bf16[1024,1024]{1,0:T(8,128)(2,1)S(1)}, bf16[1024,1024]{1,0:T(8,128)(2,1)}, u32[]{:S(2)}) %copy-start) | copy-done | bytes 2097176
  1.6 0.0 copy-start.1
  1.6 0.9 %copy-done.1 = bf16[2,1024,64]{1,2,0:T(8,128)(2,1)S(1)} copy-done((bf16[2,1024,64]{1,2,0:T(8,128)(2,1)S(1)}, bf16[2,1024,64]{1,2,0:T(8,128)(2,1)}, u32[]{:S(2)}) %copy-start.1) | copy-done | bytes 262168
  2.5 0.0 copy-start.2
  2.5 0.9 %copy-done.2 = bf16[2,64,1024]{2,1,0:T(8,128)(2,1)S(1)} copy-done((bf16[2,64,1024]{2,1,0:T(8,128)(2,1)S(1)}, bf16[2,64,1024]{2,1,0:T(8,128)(2,1)}, u32[]{:S(2)}) %copy-start.2) | copy-done | bytes 262168
  3.5 0.0 copy-start.3
  3.5 0.7 %copy-done.3 = bf16[4,1024]{1,0:T(4,128)(2,1)S(1)} copy-done((bf16[4,1024]{1,0:T(4,128)(2,1)S(1)}, bf16[4,1024]{1,0:T(4,128)(2,1)}, u32[]{:S(2)}) %copy-start.3) | copy-done | bytes 8216
  4.2 0.0 copy-start.4
  4.2 0.7 %copy-done.4 = bf16[4,1024]{1,0:T(4,128)(2,1)S(1)} copy-done((bf16[4,1024]{1,0:T(4,128)(2,1)S(1)}, bf16[4,1024]{1,0:T(4,128)(2,1)}, u32[]{:S(2)}) %copy-start.4) | copy-done | bytes 8216
  4.9 0.0 copy-start.5
  4.9 0.7 %copy-done.5 = bf16[4,1024]{1,0:T(4,128)(2,1)S(1)} copy-done((bf16[4,1024]{1,0:T(4,128)(2,1)S(1)}, bf16[4,1024]{1,0:T(4,128)(2,1)}, u32[]{:S(2)}) %copy-start.5) | copy-done | bytes 8216
  5.6 0.0 copy-start.6
  5.6 0.7 %copy-done.6 = bf16[2,1024]{1,0:T(2,128)(2,1)S(1)} copy-done((bf16[2,1024]{1,0:T(2,128)(2,1)S(1)}, bf16[2,1024]{1,0:T(2,128)(2,1)}, u32[]{:S(2)}) %copy-start.6) | copy-done | bytes 4120
  6.3 0.0 copy-start.7
  6.3 0.7 %copy-done.7 = bf16[2,64]{1,0:T(2,128)(2,1)S(1)} copy-done((bf16[2,64]{1,0:T(2,128)(2,1)S(1)}, bf16[2,64]{1,0:T(2,128)(2,1)}, u32[]{:S(2)}) %copy-start.7) | copy-done | bytes 280
  6.9 50.1 %shard_map.82 = bf16[128,1024]{1,0:T(8,128)(2,1)S(1)} custom-call(bf16[1024,1024]{1,0:T(8,128)(2,1)S(1)} %copy-done, bf16[2,64,1024]{2,1,0:T(8,128)(2,1)S(1)} %bitcast.1, bf16[2,64]{1,0:T(2,128)(2,1)S(1)} %copy-done.7, bf16[2,64,1024]{2,1,0:T(8,128)(2,1)S(1)} %copy-done.2, bf16[2,1024]{1,0:T(2,128)(2,1)S(1)} %copy-done.6, bf16[4,1024]{1,0:T(4,128)(2,1)S(1)} %copy-done.3, ...), custom_call_target="tpu_custom_call" | custom-call | tf_op jit(solution)/shard_map/pallas_call | solution.py:315
  57.1 0.7 %copy.10 = bf16[128,1024]{1,0:T(8,128)(2,1)} copy(bf16[128,1024]{1,0:T(8,128)(2,1)S(1)} %shard_map.82) | data formatting | bytes 524288
Async XLA Ops:
  0.0 1.6 %copy-start = (bf16[1024,1024]{1,0:T(8,128)(2,1)S(1)}, bf16[1024,1024]{1,0:T(8,128)(2,1)}, u32[]{:S(2)}) copy-start(bf16[1024,1024]{1,0:T(8,128)(2,1)} %tokens.1) | copy-start | bytes 6291460
  1.6 0.9 %copy-start.1 = (bf16[2,1024,64]{1,2,0:T(8,128)(2,1)S(1)}, bf16[2,1024,64]{1,2,0:T(8,128)(2,1)}, u32[]{:S(2)}) copy-start(bf16[2,1024,64]{1,2,0:T(8,128)(2,1)} %param.9) | copy-start | bytes 786436
  2.5 0.9 %copy-start.2 = (bf16[2,64,1024]{2,1,0:T(8,128)(2,1)S(1)}, bf16[2,64,1024]{2,1,0:T(8,128)(2,1)}, u32[]{:S(2)}) copy-start(bf16[2,64,1024]{2,1,0:T(8,128)(2,1)} %up_in.1) | copy-start | bytes 786436
  3.5 0.7 %copy-start.3 = (bf16[4,1024]{1,0:T(4,128)(2,1)S(1)}, bf16[4,1024]{1,0:T(4,128)(2,1)}, u32[]{:S(2)}) copy-start(bf16[4,1024]{1,0:T(4,128)(2,1)} %q_in.1) | copy-start | bytes 24580
  4.2 0.7 %copy-start.4 = (bf16[4,1024]{1,0:T(4,128)(2,1)S(1)}, bf16[4,1024]{1,0:T(4,128)(2,1)}, u32[]{:S(2)}) copy-start(bf16[4,1024]{1,0:T(4,128)(2,1)} %k_in.1) | copy-start | bytes 24580
  4.9 0.7 %copy-start.5 = (bf16[4,1024]{1,0:T(4,128)(2,1)S(1)}, bf16[4,1024]{1,0:T(4,128)(2,1)}, u32[]{:S(2)}) copy-start(bf16[4,1024]{1,0:T(4,128)(2,1)} %v_in.1) | copy-start | bytes 24580
  5.6 0.7 %copy-start.6 = (bf16[2,1024]{1,0:T(2,128)(2,1)S(1)}, bf16[2,1024]{1,0:T(2,128)(2,1)}, u32[]{:S(2)}) copy-start(bf16[2,1024]{1,0:T(2,128)(2,1)} %ub_in.1) | copy-start | bytes 12292
  6.3 0.7 %copy-start.7 = (bf16[2,64]{1,0:T(2,128)(2,1)S(1)}, bf16[2,64]{1,0:T(2,128)(2,1)}, u32[]{:S(2)}) copy-start(bf16[2,64]{1,0:T(2,128)(2,1)} %db_in.1) | copy-start | bytes 772

commit v2 on v1

--- a/solution.py
+++ b/solution.py
@@ -14,9 +14,9 @@
 
 
 class Copy:
-    def __init__(self, name, region, step, needs, size, front=0.0):
+    def __init__(self, name, region, step, needs, size):
         self.name, self.region, self.step = name, region, step
-        self.needs, self.size, self.front = needs, size, front
+        self.needs, self.size = needs, size
 
 
 class Work:
@@ -24,37 +24,64 @@
         self.name, self.run, self.needs, self.cost = name, run, needs, cost
 
 
+def up_from(k):
+    if k == 4:
+        return [("up", 0, 1, 4), ("up", 1, -1, 4)]
+    way = 1 if k < 0 else -1
+    return [("up", half, way, abs(k)) for half in range(2)]
+
+
 def plan_copies():
     copies = {}
 
-    def add(name, region, step, needs, size, front=0.0):
-        copies[name] = Copy(name, region, step, tuple(needs), size, front)
+    def add(name, region, step, needs, size):
+        copies[name] = Copy(name, region, step, tuple(needs), size)
+
+    def reach(name, region, size, way):
+        for d in (2, -2, 1, -1):
+            add((*name, d), region(0), (0, 0, 0, d), (), size)
+        for d in (3, -3):
+            sign = d // 3
+            add((*name, d), region(-2 * sign), (0, 0, 0, sign), [(*name, 2 * sign)], size)
+        add((*name, 4), region(-2 * way), (0, 0, 0, 2 * way), [(*name, 2 * way)], size)
 
     def page(m):
-        return lambda r, x, y, c, z: r["w"].at[m, x, y, c, pl.ds(4 * z, 4)]
+        return lambda back: lambda r, x, y, c, z: r["w"].at[m, x, y, c, pl.ds(4 * ((z + back + NZ) % NZ), 4)]
 
     for m in range(3):
-        for d in Z_STEPS:
-            add(("page", m, d), page(m), (0, 0, 0, d), (), 8)
-    for d in Z_STEPS:
-        add(("ub", d), lambda r, x, y, c, z: r["ub"].at[z], (0, 0, 0, d), (), 4)
-        add(("db", d), lambda r, x, y, c, z: r["db"].at[z], (0, 0, 0, d), (), 1)
-
-    def ring(buf, back):
-        return lambda r, x, y, c, z: r[buf].at[(z + back + NZ) % NZ, c]
+        reach(("page", m), page(m), 8, (1, -1, 1)[m])
+    reach(("ub",), lambda back: lambda r, x, y, c, z: r["ub"].at[(z + back + NZ) % NZ], 4, -1)
+
+    def ring(half, back):
+        return lambda r, x, y, c, z: r["up"].at[(z + back + NZ) % NZ, c, pl.ds(32 * half, 32)]
 
     for s in range(1, 5):
-        for buf, way in (("dn", 1), ("up", -1), ("up", 1), ("dn", -1)):
-            if s == 4 and (buf, way) in (("up", 1), ("dn", -1)):
+        for half, way in ((0, 1), (1, -1), (1, 1), (0, -1)):
+            if s == 4 and (half, way) in ((1, 1), (0, -1)):
                 continue
-            needs = [("ring", buf, way, s - 1)] if s > 1 else []
-            add(("ring", buf, way, s), ring(buf, -way * (s - 1)), (0, 0, 0, way), needs, 128)
-    for buf in ("dn", "up"):
-        for k in (-1, 1, -2, 2, -3, 3, 4):
-            src = ("ring", buf, 1, -k) if k < 0 else ("ring", buf, -1, k)
-            if k == 4 and buf == "dn":
-                src = ("ring", "dn", 1, 4)
-            add(("pair", buf, k), ring(buf, k), (0, 0, 1, 0), [src], 128)
+            needs = [("up", half, way, s - 1)] if s > 1 else []
+            add(("up", half, way, s), ring(half, -way * (s - 1)), (0, 0, 0, way), needs, 64)
+
+    def hidden(src, dst, lo, rows):
+        return lambda r, x, y, c, z: r["hb"].at[(z + src + NZ) % NZ, (z + dst + NZ) % NZ, pl.ds(lo, rows)]
+
+    for sign in (1, -1):
+        lo = 0 if sign == 1 else 64
+        add(("hop", 4, lo), hidden(0, 4, lo, 64), (0, 0, 0, 2 * sign), ["h"], 16)
+        add(("hop", 3 * sign), hidden(0, 3 * sign, 0, 128), (0, 0, 0, 2 * sign), ["h"], 32)
+    for sign in (1, -1):
+        for d in (2, 1):
+            add(("hid", d * sign), hidden(0, d * sign, 0, 128), (0, 0, 0, d * sign), ["h"], 32)
+    for sign in (1, -1):
+        lo = 0 if sign == 1 else 64
+        add(("hid", 3 * sign), hidden(-2 * sign, sign, 0, 128), (0, 0, 0, sign), [("hop", 3 * sign)], 32)
+        add(("hid", 4, lo), hidden(-2 * sign, 2 * sign, lo, 64), (0, 0, 0, 2 * sign), [("hop", 4, lo)], 16)
+
+    def whole(k):
+        return lambda r, x, y, c, z: r["up"].at[(z + k + NZ) % NZ, c]
+
+    for k in (-1, 1, -2, 2, -3, 3, 4):
+        add(("pair", k), whole(k), (0, 0, 1, 0), up_from(k), 128)
 
     def block(m, h, i, j, lo, rows):
         def at(r, x, y, c, z):
@@ -103,7 +130,9 @@
             for d in (1, -1):
                 got = [("s3", key, i, d) for i in (0, -1, 1, 2)]
                 add(("hand", key, -d), line(m, h, -d, 0, 16), (0, 0, 1, 0), got, 128)
-            add(("hand", key, 2), line(m, h, 2, 0, 16), (0, 0, 1, 0), [("s4", key, 1), ("s4", key, -1)], 128)
+            for d in (1, -1):
+                lo = 0 if d == 1 else 8
+                add(("hand", key, 2, d), line(m, h, 2, lo, 8), (0, 0, 1, 0), [("s4", key, d)], 64)
     return copies
 
 
@@ -114,21 +143,15 @@
         names += [("s1", key, d) for d in (1, -1)] + [("s2", key, d) for d in (1, -1)]
         names += [("s3", key, i, d) for i in (0, -1, 1, 2) for d in (1, -1)]
         names += [("s4", key, d) for d in (1, -1)]
-        names += [("hand", key, j) for j in (0, 1, -1, 2)]
+        names += [("hand", key, j) for j in (0, 1, -1)] + [("hand", key, 2, d) for d in (1, -1)]
     return names
 
 
 def pair_needs(k):
     if k == 0:
-        return []
-    d = -k if k != 4 else 4
-    names = [("ub", d), ("db", d), ("pair", "dn", k), ("pair", "up", k)]
-    for buf in ("dn", "up"):
-        src = ("ring", buf, 1, -k) if k < 0 else ("ring", buf, -1, k)
-        if k == 4 and buf == "dn":
-            src = ("ring", "dn", 1, 4)
-        names.append(src)
-    return names
+        return ["h"]
+    hid = [("hid", 4, 0), ("hid", 4, 64)] if k == 4 else [("hid", -k)]
+    return [("ub", 4 if k == 4 else -k), ("pair", k), *hid, *up_from(k)]
 
 
 def plan_order(copies, works):
@@ -141,13 +164,13 @@
             moved = False
             for name in list(unsent):
                 c = copies[name]
-                if all(n in waited for n in c.needs):
+                if all(n in waited or n in done for n in c.needs):
                     axis = next(i for i in range(4) if c.step[i])
                     hops = abs(c.step[axis])
                     if axis == 2:
                         link, rate, late = "core", 620.0, 0.9
                     else:
-                        link, rate, late = (axis, c.step[axis] > 0), 45.0, 0.95 + 0.8 * hops
+                        link, rate, late = (axis, c.step[axis] > 0), 41.0, 0.95 + 0.8 * hops
                     begin = max(now, free.get(link, 0.0))
                     took = c.size * 1.024 / rate * hops
                     free[link] = begin + took
@@ -176,11 +199,11 @@
 
 
 def kernel(
-    copies, tokens, dn_in, db_in, up_in, ub_in, q_in, k_in, v_in, out, xs, w, dn, up, db, ub, ad, qhl, qk, mix, loc, ss, rs
+    copies, tokens, dn_in, db_in, up_in, ub_in, q_in, k_in, v_in, out, xa, xs, w, dn, up, db, ub, hb, ad, qhl, qk, sc, mix, loc, ss, rs
 ):
     dp, z = lax.axis_index("dp"), lax.axis_index("adapter")
     x, y, c = dp // 8, (dp // 2) % 4, dp % 2
-    refs = {"w": w, "dn": dn, "up": up, "db": db, "ub": ub}
+    refs = {"w": w, "up": up, "ub": ub, "hb": hb}
     ids = {name: i for i, name in enumerate(copies)}
 
     own = [
@@ -188,9 +211,10 @@
         (k_in, w.at[1, x, y, c, pl.ds(4 * z, 4)]),
         (v_in, w.at[2, x, y, c, pl.ds(4 * z, 4)]),
         (ub_in, ub.at[z]),
-        (db_in, db.at[z]),
-        (dn_in, dn.at[z]),
         (up_in, up.at[z]),
+        (db_in, db),
+        (dn_in, dn),
+        (tokens, xa),
         (tokens.at[pl.ds(128 * z, 128)], xs),
     ]
     own = [pltpu.make_async_copy(a, b, loc.at[i]) for i, (a, b) in enumerate(own)]
@@ -219,7 +243,7 @@
             device_id_type=pl.DeviceIdType.MESH,
         )
 
-    peers = [(0, 0, 0, d) for d in Z_STEPS] + [(1, 0, 0, 0), (-1, 0, 0, 0), (0, 1, 0, 0), (0, -1, 0, 0), (0, 0, 1, 0)]
+    peers = [(0, 0, 0, d) for d in (1, -1, 2, -2)] + [(1, 0, 0, 0), (-1, 0, 0, 0), (0, 1, 0, 0), (0, -1, 0, 0), (0, 0, 1, 0)]
     barrier = pltpu.get_barrier_semaphore()
     for step in peers:
         pl.semaphore_signal(barrier, inc=1, device_id=device(step), device_id_type=pl.DeviceIdType.MESH)
@@ -227,13 +251,21 @@
     for cp in own:
         cp.wait()
 
+    def hide():
+        bias = db[...].astype(F32)
+        bias = jnp.concatenate([bias[0:1], bias[1:2]], axis=1)
+        both = dn.reshape(128, 1024)
+
+        @pl.loop(0, NZ)
+        def _(to):
+            rows = xa[pl.ds(pl.multiple_of(to * 128, 128), 128), :]
+            raised = lax.dot_general(rows, both[...], NT, preferred_element_type=F32)
+            hb[z, to] = jnp.maximum(raised + bias, 0.0).astype(BF16)
+
     def adapters(k):
         def run():
             at = (z + k + NZ) % NZ
-            bias = db[at].astype(F32)
-            bias = jnp.concatenate([bias[0:1], bias[1:2]], axis=1)
-            hid = lax.dot_general(xs[...], dn[at].reshape(128, 1024), NT, preferred_element_type=F32)
-            hid = jnp.maximum(hid + bias, 0.0).astype(BF16)
+            hid = hb[at, z]
             lift = ub[at].astype(F32)
             for i in range(2):
                 for n in range(4):
@@ -245,6 +277,19 @@
 
         return run
 
+    def score(k):
+        def run():
+            first = 2 * ((k + NZ) % NZ)
+
+            @pl.loop(0, 8)
+            def _(step):
+                rows = pl.ds(pl.multiple_of(step * 16, 16), 16)
+                weight = qk[rows, :]
+                for a in (first, first + 1):
+                    sc[a, rows, :] = jnp.sum(ad[a, rows, :].astype(F32) * weight, axis=1, keepdims=True)
+
+        return run
+
     def split(part, rows, cols, value):
         high = value.astype(BF16)
         part[rows, cols] = high
@@ -268,8 +313,7 @@
         @pl.loop(0, 8)
         def _(step):
             rows = pl.ds(pl.multiple_of(step * 16, 16), 16)
-            weight = qk[rows, :]
-            scores = [jnp.sum(ad[a, rows, :].astype(F32) * weight, axis=1, keepdims=True) for a in range(16)]
+            scores = [sc[a, rows, :] for a in range(16)]
             peak = functools.reduce(jnp.maximum, scores)
             scores = [jnp.exp(s - peak) for s in scores]
             scale = 1.0 / functools.reduce(jnp.add, scores)
@@ -288,14 +332,12 @@
             both = jnp.dot(mix[...], whole[:, cols], preferred_element_type=F32)
             out[:, cols] = (xs[:, cols].astype(F32) + both[:128] + both[128:]).astype(BF16)
 
-    works = [
-        Work("q", query, all_of(0), 0.6),
-        Work("k", key, ["q"] + all_of(1), 0.8),
-    ]
     pairs = [0, -1, 1, -2, 2, -3, 3, 4]
-    works += [Work(("a", k), adapters(k), pair_needs(k), 0.6) for k in pairs]
-    works.append(Work("s", attend, ["k"] + [("a", k) for k in pairs], 3.0))
-    works.append(Work("v", value, ["s"] + all_of(2), 0.8))
+    works = [Work("h", hide, [], 1.3), Work("q", query, all_of(0), 0.6), Work("k", key, ["q"] + all_of(1), 0.8)]
+    works += [Work(("a", k), adapters(k), pair_needs(k), 0.5) for k in pairs]
+    works += [Work(("s", k), score(k), ["k", ("a", k)], 0.3) for k in pairs]
+    works.append(Work("m", attend, [("s", k) for k in pairs], 1.5))
+    works.append(Work("v", value, ["m"] + all_of(2), 0.8))
     by_name = {job.name: job for job in works}
     order, _ = plan_order(copies, works)
     for kind, name in order:
@@ -311,29 +353,32 @@
 
 def body(tokens, down_weight, down_bias, up_weight, up_bias, query_weight, key_weight, value_weight):
     copies = plan_copies()
-    hbm = pl.BlockSpec(memory_space=pl.ANY)
+    hbm = pl.BlockSpec(memory_space=pltpu.HBM)
     return pl.pallas_call(
         functools.partial(kernel, copies),
         out_shape=jax.ShapeDtypeStruct((128, 1024), BF16),
         in_specs=[hbm] * 8,
         out_specs=pl.BlockSpec(memory_space=pltpu.VMEM),
         scratch_shapes=[
+            pltpu.VMEM((1024, 1024), BF16),
             pltpu.VMEM((128, 1024), BF16),
             pltpu.VMEM((3, NX, NY, NC, 32, 1024), BF16),
+            pltpu.VMEM((2, 64, 1024), BF16),
             pltpu.VMEM((NZ, 2, 64, 1024), BF16),
-            pltpu.VMEM((NZ, 2, 64, 1024), BF16),
-            pltpu.VMEM((NZ, 2, 64), BF16),
+            pltpu.VMEM((2, 64), BF16),
             pltpu.VMEM((NZ, 2, 1024), BF16),
+            pltpu.VMEM((NZ, NZ, 128, 128), BF16),
             pltpu.VMEM((16, 128, 1024), BF16),
             pltpu.VMEM((256, 1024), BF16),
             pltpu.VMEM((128, 1024), F32),
+            pltpu.VMEM((16, 128, 1), F32),
             pltpu.VMEM((256, 1024), BF16),
-            pltpu.SemaphoreType.DMA((8,)),
+            pltpu.SemaphoreType.DMA((9,)),
             pltpu.SemaphoreType.DMA((len(copies),)),
             pltpu.SemaphoreType.DMA((len(copies),)),
         ],
         compiler_params=pltpu.CompilerParams(
-            collective_id=0, has_side_effects=True, vmem_limit_bytes=48 * 1024 * 1024
+            collective_id=0, has_side_effects=True, vmem_limit_bytes=67043328
         ),
     )(
         tokens,

time: 58.1 us -> 56.8 us (0.978)
  local copies, waits for them, and re-layouts: 7.62 us -> 1.67 us
  Pallas kernels: 50.1 us -> 55 us
    unnamed x17 -> x1, local copies, waits for them, and re-layouts: 7.62 us -> 1.67 us
    pallas_call x1, Pallas kernels: 50.1 us -> 55 us  [body(): pl.pallas_call(functools.partial(kernel, copies), out_shape=jax.ShapeDtyp...]
where the time goes in v2:
time: 56.8 us; the launch traced here: 56.7 us
  Pallas kernels  55 us (97%)
  local copies, waits for them, and re-layouts  1.67 us (3%)
    pallas_call x1, Pallas kernels, body(): pl.pallas_call(functools.partial(kernel, copies), out_shape=jax.ShapeDtyp...  55 us
    unnamed x1, local copies, waits for them, and re-layouts  1.67 us

profile of v2, /device:TPU:1, one launch (start us, length us, event | category | flops | bytes accessed | tf_op | source)
XLA Modules:
  0.0 56.7 jit_solution(2744137605575284010)
XLA Ops:
  0.0 55.0 %shard_map.82 = bf16[128,1024]{1,0:T(8,128)(2,1)} custom-call(bf16[1024,1024]{1,0:T(8,128)(2,1)} %tokens.1, bf16[2,64,1024]{2,1,0:T(8,128)(2,1)} %bitcast.1, bf16[2,64]{1,0:T(2,128)(2,1)} %db_in.1, bf16[2,64,1024]{2,1,0:T(8,128)(2,1)} %up_in.1, bf16[2,1024]{1,0:T(2,128)(2,1)} %ub_in.1, bf16[4,1024]{1,0:T(4,128)(2,1)} %q_in.1, bf16[4,1024]{1,0:T(4,128)(2,1)} %k_in.1, ...), custom_call_target="tpu_custom_call" | custom-call | tf_op jit(solution)/shard_map/pallas_call | solution.py:357
  55.0 1.7 %copy.10 = bf16[128,1024]{1,0:T(8,128)(2,1)} copy(bf16[128,1024]{1,0:T(8,128)(2,1)} %shard_map.82) | data formatting | bytes 524288

commit v3 on v2

--- a/solution.py
+++ b/solution.py
@@ -154,31 +154,44 @@
     return [("ub", 4 if k == 4 else -k), ("pair", k), *hid, *up_from(k)]
 
 
-def plan_order(copies, works):
+def urgency(name):
+    kind = name[0]
+    if kind == "page":
+        return (0, name[1], 0)
+    if kind in ("ub", "up", "hop", "hid", "pair"):
+        return (1, {"hop": 0, "up": 1, "hid": 2, "ub": 3, "pair": 4}[kind], 0)
+    return (2 + name[1][0], {"s1": 0, "s2": 1, "s3": 2, "s4": 3, "hand": 4}[kind], 0)
+
+
+def plan_order(copies, works, backlog=2.0):
     free, arrival, order = {}, {}, []
     now, waited, done = 0.0, set(), set()
-    unsent, todo = list(copies), list(works)
+    unsent, todo = sorted(copies, key=urgency), list(works)
+
+    def route(c):
+        axis = next(i for i in range(4) if c.step[i])
+        hops = abs(c.step[axis])
+        if axis == 2:
+            return "core", c.size / 600.0, 0.9
+        return (axis, c.step[axis] > 0), c.size * hops / 41.0, 0.95 + 0.8 * hops
+
+    def start_ready(until):
+        nonlocal now
+        for name in list(unsent):
+            c = copies[name]
+            if all(n in waited or n in done for n in c.needs):
+                link, took, late = route(c)
+                if free.get(link, 0.0) - until > backlog:
+                    continue
+                begin = max(now, free.get(link, 0.0))
+                free[link] = begin + took
+                arrival[name] = begin + took + late
+                order.append(("start", name))
+                unsent.remove(name)
+                now += 0.01
+
     while True:
-        moved = True
-        while moved:
-            moved = False
-            for name in list(unsent):
-                c = copies[name]
-                if all(n in waited or n in done for n in c.needs):
-                    axis = next(i for i in range(4) if c.step[i])
-                    hops = abs(c.step[axis])
-                    if axis == 2:
-                        link, rate, late = "core", 620.0, 0.9
-                    else:
-                        link, rate, late = (axis, c.step[axis] > 0), 41.0, 0.95 + 0.8 * hops
-                    begin = max(now, free.get(link, 0.0))
-                    took = c.size * 1.024 / rate * hops
-                    free[link] = begin + took
-                    arrival[name] = begin + took + late
-                    order.append(("start", name))
-                    unsent.remove(name)
-                    now += 0.01
-                    moved = True
+        start_ready(now)
         ready = sorted((t, i, n) for i, (n, t) in enumerate(arrival.items()) if n not in waited)
         if ready and ready[0][0] <= now:
             order.append(("wait", ready[0][2]))
@@ -193,7 +206,9 @@
             continue
         if not ready:
             break
-        now = ready[0][0]
+        start_ready(ready[0][0])
+        ready = sorted((t, i, n) for i, (n, t) in enumerate(arrival.items()) if n not in waited)
+        now = max(now, ready[0][0])
     assert not unsent and not todo
     return order, now
 
@@ -248,10 +263,12 @@
     for step in peers:
         pl.semaphore_signal(barrier, inc=1, device_id=device(step), device_id_type=pl.DeviceIdType.MESH)
     pl.semaphore_wait(barrier, len(peers))
-    for cp in own:
+    for cp in own[:5]:
         cp.wait()
 
     def hide():
+        for cp in own[5:]:
+            cp.wait()
         bias = db[...].astype(F32)
         bias = jnp.concatenate([bias[0:1], bias[1:2]], axis=1)
         both = dn.reshape(128, 1024)
@@ -280,13 +297,12 @@
     def score(k):
         def run():
             first = 2 * ((k + NZ) % NZ)
-
-            @pl.loop(0, 8)
-            def _(step):
-                rows = pl.ds(pl.multiple_of(step * 16, 16), 16)
-                weight = qk[rows, :]
-                for a in (first, first + 1):
-                    sc[a, rows, :] = jnp.sum(ad[a, rows, :].astype(F32) * weight, axis=1, keepdims=True)
+            for a in (first, first + 1):
+                total = ad[a, :, :128].astype(F32) * qk[:, :128]
+                for n in range(1, 8):
+                    cols = slice(128 * n, 128 * n + 128)
+                    total = total + ad[a, :, cols].astype(F32) * qk[:, cols]
+                sc[:, a : a + 1] = jnp.sum(total, axis=1, keepdims=True)
 
         return run
 
@@ -310,20 +326,15 @@
             qk[:, cols] = (both[:128] + both[128:]) * (1.0 / 32.0)
 
     def attend():
-        @pl.loop(0, 8)
-        def _(step):
-            rows = pl.ds(pl.multiple_of(step * 16, 16), 16)
-            scores = [sc[a, rows, :] for a in range(16)]
-            peak = functools.reduce(jnp.maximum, scores)
-            scores = [jnp.exp(s - peak) for s in scores]
-            scale = 1.0 / functools.reduce(jnp.add, scores)
-            total = scores[0] * ad[0, rows, :].astype(F32)
+        weight = sc[:, :16]
+        weight = jnp.exp(weight - jnp.max(weight, axis=1, keepdims=True))
+        weight = weight / jnp.sum(weight, axis=1, keepdims=True)
+        for row in range(0, 128, 16):
+            rows = slice(row, row + 16)
+            total = weight[rows, :1] * ad[0, rows, :].astype(F32)
             for a in range(1, 16):
-                total = total + scores[a] * ad[a, rows, :].astype(F32)
-            total = total * scale
-            high = total.astype(BF16)
-            mix[rows, :] = high
-            mix[pl.ds(pl.multiple_of(step * 16 + 128, 16), 16), :] = (total - high.astype(F32)).astype(BF16)
+                total = total + weight[rows, a : a + 1] * ad[a, rows, :].astype(F32)
+            split(mix, rows, slice(None), total)
 
     def value():
         whole = w.at[2].reshape(1024, 1024)
@@ -371,7 +382,7 @@
             pltpu.VMEM((16, 128, 1024), BF16),
             pltpu.VMEM((256, 1024), BF16),
             pltpu.VMEM((128, 1024), F32),
-            pltpu.VMEM((16, 128, 1), F32),
+            pltpu.VMEM((128, 16), F32),
             pltpu.VMEM((256, 1024), BF16),
             pltpu.SemaphoreType.DMA((9,)),
             pltpu.SemaphoreType.DMA((len(copies),)),

time: 56.8 us -> 47 us (0.83)
  Pallas kernels: 55 us -> 45.2 us
    pallas_call x1, Pallas kernels: 55 us -> 45.2 us  [body(): pl.pallas_call(functools.partial(kernel, copies), out_shape=jax.ShapeDtyp...]
where the time goes in v3:
time: 47 us; the launch traced here: 46.9 us
  Pallas kernels  45.2 us (96%)
  local copies, waits for them, and re-layouts  1.67 us (4%)
    pallas_call x1, Pallas kernels, body(): pl.pallas_call(functools.partial(kernel, copies), out_shape=jax.ShapeDtyp...  45.2 us
    unnamed x1, local copies, waits for them, and re-layouts  1.67 us

profile of v3, /device:TPU:1, one launch (start us, length us, event | category | flops | bytes accessed | tf_op | source)
XLA Modules:
  0.0 46.9 jit_solution(11679597052675141827)
XLA Ops:
  0.0 45.2 %shard_map.82 = bf16[128,1024]{1,0:T(8,128)(2,1)} custom-call(bf16[1024,1024]{1,0:T(8,128)(2,1)} %tokens.1, bf16[2,64,1024]{2,1,0:T(8,128)(2,1)} %bitcast.1, bf16[2,64]{1,0:T(2,128)(2,1)} %db_in.1, bf16[2,64,1024]{2,1,0:T(8,128)(2,1)} %up_in.1, bf16[2,1024]{1,0:T(2,128)(2,1)} %ub_in.1, bf16[4,1024]{1,0:T(4,128)(2,1)} %q_in.1, bf16[4,1024]{1,0:T(4,128)(2,1)} %k_in.1, ...), custom_call_target="tpu_custom_call" | custom-call | tf_op jit(solution)/shard_map/pallas_call | solution.py:368
  45.2 1.7 %copy.10 = bf16[128,1024]{1,0:T(8,128)(2,1)} copy(bf16[128,1024]{1,0:T(8,128)(2,1)} %shard_map.82) | data formatting | bytes 524288

commit v4 on v3

--- a/solution.py
+++ b/solution.py
@@ -163,7 +163,7 @@
     return (2 + name[1][0], {"s1": 0, "s2": 1, "s3": 2, "s4": 3, "hand": 4}[kind], 0)
 
 
-def plan_order(copies, works, backlog=2.0):
+def plan_order(copies, works, backlog=2.0, margin=1.5):
     free, arrival, order = {}, {}, []
     now, waited, done = 0.0, set(), set()
     unsent, todo = sorted(copies, key=urgency), list(works)
@@ -190,26 +190,44 @@
                 unsent.remove(name)
                 now += 0.01
 
+    feeds = {n for c in copies.values() for n in c.needs}
+
+    def when(work):
+        times = [0.0]
+        for n in work.needs:
+            if n in waited or n in done:
+                continue
+            if n in feeds or n not in arrival:
+                return None
+            times.append(arrival[n] + margin)
+        return max(times)
+
     while True:
         start_ready(now)
-        ready = sorted((t, i, n) for i, (n, t) in enumerate(arrival.items()) if n not in waited)
-        if ready and ready[0][0] <= now:
-            order.append(("wait", ready[0][2]))
-            waited.add(ready[0][2])
+        relays = sorted((arrival[n], i, n) for i, n in enumerate(arrival) if n in feeds and n not in waited)
+        if relays and relays[0][0] <= now:
+            order.append(("wait", relays[0][2]))
+            waited.add(relays[0][2])
             continue
-        run = next((w for w in todo if all(n in waited or n in done for n in w.needs)), None)
-        if run is not None:
-            order.append(("work", run.name))
-            now += run.cost
-            done.add(run.name)
-            todo.remove(run)
+        times = [(when(w), i) for i, w in enumerate(todo) if when(w) is not None]
+        run = next((i for t, i in times if t <= now), None)
+        if run is None:
+            following = [t for t, _ in times] + [t for t, _, _ in relays]
+            if not following:
+                break
+            start_ready(min(following))
+            now = max(now, min(following))
             continue
-        if not ready:
-            break
-        start_ready(ready[0][0])
-        ready = sorted((t, i, n) for i, (n, t) in enumerate(arrival.items()) if n not in waited)
-        now = max(now, ready[0][0])
+        run = todo.pop(run)
+        for n in run.needs:
+            if n in copies and n not in waited:
+                order.append(("wait", n))
+                waited.add(n)
+        order.append(("work", run.name))
+        now += run.cost
+        done.add(run.name)
     assert not unsent and not todo
+    order += [("wait", n) for n in copies if n not in waited]
     return order, now
 
 

time: 47 us -> 46.1 us (0.981)
  Pallas kernels: 45.2 us -> 44.3 us
    pallas_call x1, Pallas kernels: 45.2 us -> 44.3 us  [body(): pl.pallas_call(functools.partial(kernel, copies), out_shape=jax.ShapeDtyp...]
where the time goes in v4:
time: 46.1 us; the launch traced here: 45.9 us
  Pallas kernels  44.3 us (96%)
  local copies, waits for them, and re-layouts  1.67 us (4%)
    pallas_call x1, Pallas kernels, body(): pl.pallas_call(functools.partial(kernel, copies), out_shape=jax.ShapeDtyp...  44.3 us
    unnamed x1, local copies, waits for them, and re-layouts  1.67 us

profile of v4, /device:TPU:1, one launch (start us, length us, event | category | flops | bytes accessed | tf_op | source)
XLA Modules:
  0.0 45.9 jit_solution(17793237252272704329)
XLA Ops:
  0.0 44.3 %shard_map.82 = bf16[128,1024]{1,0:T(8,128)(2,1)} custom-call(bf16[1024,1024]{1,0:T(8,128)(2,1)} %tokens.1, bf16[2,64,1024]{2,1,0:T(8,128)(2,1)} %bitcast.1, bf16[2,64]{1,0:T(2,128)(2,1)} %db_in.1, bf16[2,64,1024]{2,1,0:T(8,128)(2,1)} %up_in.1, bf16[2,1024]{1,0:T(2,128)(2,1)} %ub_in.1, bf16[4,1024]{1,0:T(4,128)(2,1)} %q_in.1, bf16[4,1024]{1,0:T(4,128)(2,1)} %k_in.1, ...), custom_call_target="tpu_custom_call" | custom-call | tf_op jit(solution)/shard_map/pallas_call | solution.py:386
  44.3 1.7 %copy.10 = bf16[128,1024]{1,0:T(8,128)(2,1)} copy(bf16[128,1024]{1,0:T(8,128)(2,1)} %shard_map.82) | data formatting | bytes 524288

commit v5 on v4

--- a/solution.py
+++ b/solution.py
@@ -10,6 +10,10 @@
 BF16, F32 = jnp.bfloat16, jnp.float32
 NX, NY, NC, NZ = 4, 4, 2, 8
 Z_STEPS = (4, 3, -3, 2, -2, 1, -1)
+ORDER_Z = ("hop", "up", "hid", "ub", "pair")
+ORDER_XY = ("s1", "s2", "s3", "s4", "hand")
+MATRIX, MARGIN, BACKLOG, BACKLOG_Z = 10, 1.5, 2.0, 2.0
+RATE, RATE_Z, LATE, COST = 41.0, 41.0, 0.95, 1.0
 NT = (((1,), (1,)), ((), ()))
 
 
@@ -159,11 +163,11 @@
     if kind == "page":
         return (0, name[1], 0)
     if kind in ("ub", "up", "hop", "hid", "pair"):
-        return (1, {"hop": 0, "up": 1, "hid": 2, "ub": 3, "pair": 4}[kind], 0)
-    return (2 + name[1][0], {"s1": 0, "s2": 1, "s3": 2, "s4": 3, "hand": 4}[kind], 0)
-
-
-def plan_order(copies, works, backlog=2.0, margin=1.5):
+        return (1, ORDER_Z.index(kind), 0)
+    return (2, MATRIX * name[1][0] + ORDER_XY.index(kind), name[1][0])
+
+
+def plan_order(copies, works, margin=MARGIN):
     free, arrival, order = {}, {}, []
     now, waited, done = 0.0, set(), set()
     unsent, todo = sorted(copies, key=urgency), list(works)
@@ -173,7 +177,7 @@
         hops = abs(c.step[axis])
         if axis == 2:
             return "core", c.size / 600.0, 0.9
-        return (axis, c.step[axis] > 0), c.size * hops / 41.0, 0.95 + 0.8 * hops
+        return (axis, c.step[axis] > 0), c.size * hops / (RATE_Z if axis == 3 else RATE), LATE + 0.8 * hops
 
     def start_ready(until):
         nonlocal now
@@ -181,7 +185,7 @@
             c = copies[name]
             if all(n in waited or n in done for n in c.needs):
                 link, took, late = route(c)
-                if free.get(link, 0.0) - until > backlog:
+                if free.get(link, 0.0) - until > (BACKLOG_Z if link[0] == 3 else BACKLOG):
                     continue
                 begin = max(now, free.get(link, 0.0))
                 free[link] = begin + took
@@ -224,7 +228,7 @@
                 order.append(("wait", n))
                 waited.add(n)
         order.append(("work", run.name))
-        now += run.cost
+        now += run.cost * COST
         done.add(run.name)
     assert not unsent and not todo
     order += [("wait", n) for n in copies if n not in waited]
@@ -251,8 +255,6 @@
         (tokens.at[pl.ds(128 * z, 128)], xs),
     ]
     own = [pltpu.make_async_copy(a, b, loc.at[i]) for i, (a, b) in enumerate(own)]
-    for cp in own:
-        cp.start()
 
     def there(step, sign):
         px, py, pz = (x + sign * step[0] + 4) % 4, (y + sign * step[1] + 4) % 4, (z + sign * step[3] + NZ) % NZ
@@ -280,9 +282,16 @@
     barrier = pltpu.get_barrier_semaphore()
     for step in peers:
         pl.semaphore_signal(barrier, inc=1, device_id=device(step), device_id_type=pl.DeviceIdType.MESH)
+    for cp in own:
+        cp.start()
     pl.semaphore_wait(barrier, len(peers))
-    for cp in own[:5]:
-        cp.wait()
+    sources = {("page", 0): 0, ("page", 1): 1, ("page", 2): 2, ("ub",): 3, ("up",): 4}
+
+    def filled(name):
+        for kind in (name[:1], name[:2]):
+            if kind in sources:
+                own[sources.pop(kind)].wait()
+
 
     def hide():
         for cp in own[5:]:
@@ -371,10 +380,14 @@
     order, _ = plan_order(copies, works)
     for kind, name in order:
         if kind == "start":
+            filled(name)
             descriptor(name, (x, y, c, z)).start()
         elif kind == "wait":
             descriptor(name, there(copies[name].step, -1)).wait_recv()
         else:
+            if name[0] == "a":
+                filled(("ub",))
+                filled(("up",))
             by_name[name].run()
     for name in copies:
         descriptor(name, (x, y, c, z)).wait_send()
@@ -407,17 +420,22 @@
             pltpu.SemaphoreType.DMA((len(copies),)),
         ],
         compiler_params=pltpu.CompilerParams(
-            collective_id=0, has_side_effects=True, vmem_limit_bytes=67043328
+            collective_id=0, has_side_effects=True, vmem_limit_bytes=32 * 1024 * 1024
         ),
     )(
-        tokens,
-        jnp.swapaxes(down_weight, 1, 2),
-        down_bias,
-        up_weight,
-        up_bias,
-        query_weight,
-        key_weight,
-        value_weight,
+        *(
+            pltpu.with_memory_space_constraint(a, pltpu.HBM)
+            for a in (
+                tokens,
+                jnp.swapaxes(down_weight, 1, 2),
+                down_bias,
+                up_weight,
+                up_bias,
+                query_weight,
+                key_weight,
+                value_weight,
+            )
+        )
     )
 
 

time: 46.1 us -> 44.3 us (0.961)
  local copies, waits for them, and re-layouts: 1.67 us -> 0.71 us
  Pallas kernels: 44.3 us -> 43.5 us
    unnamed x1, local copies, waits for them, and re-layouts: 1.67 us -> 0.71 us
    pallas_call x1, Pallas kernels: 44.3 us -> 43.5 us  [body(): pl.pallas_call(functools.partial(kernel, copies), out_shape=jax.ShapeDtyp...]
where the time goes in v5:
time: 44.3 us; the launch traced here: 44.2 us
  Pallas kernels  43.5 us (98%)
  local copies, waits for them, and re-layouts  0.71 us (2%)
    pallas_call x1, Pallas kernels, body(): pl.pallas_call(functools.partial(kernel, copies), out_shape=jax.ShapeDtyp...  43.5 us

profile of v5, /device:TPU:1, one launch (start us, length us, event | category | flops | bytes accessed | tf_op | source)
XLA Modules:
  0.0 44.2 jit_solution(11229547349376837057)
XLA Ops:
  0.0 43.5 %shard_map.82 = bf16[128,1024]{1,0:T(8,128)(2,1)S(1)} custom-call(bf16[1024,1024]{1,0:T(8,128)(2,1)} %tokens.1, bf16[2,64,1024]{2,1,0:T(8,128)(2,1)} %bitcast.1, bf16[2,64]{1,0:T(2,128)(2,1)} %db_in.1, bf16[2,64,1024]{2,1,0:T(8,128)(2,1)} %up_in.1, bf16[2,1024]{1,0:T(2,128)(2,1)} %ub_in.1, bf16[4,1024]{1,0:T(4,128)(2,1)} %q_in.1, bf16[4,1024]{1,0:T(4,128)(2,1)} %k_in.1, ...), custom_call_target="tpu_custom_call" | custom-call | tf_op jit(solution)/shard_map/pallas_call | solution.py:399
  43.5 0.7 %copy.10 = bf16[128,1024]{1,0:T(8,128)(2,1)} copy(bf16[128,1024]{1,0:T(8,128)(2,1)S(1)} %shard_map.82) | data formatting | bytes 524288

commit v6 on v5

--- a/solution.py
+++ b/solution.py
@@ -11,9 +11,9 @@
 NX, NY, NC, NZ = 4, 4, 2, 8
 Z_STEPS = (4, 3, -3, 2, -2, 1, -1)
 ORDER_Z = ("hop", "up", "hid", "ub", "pair")
-ORDER_XY = ("s1", "s2", "s3", "s4", "hand")
-MATRIX, MARGIN, BACKLOG, BACKLOG_Z = 10, 1.5, 2.0, 2.0
-RATE, RATE_Z, LATE, COST = 41.0, 41.0, 0.95, 1.0
+ORDER_XY = ("s1", "s2", "s4", "s3", "hand")
+MATRIX, MARGIN, BACKLOG, BACKLOG_Z = 10, 1.0, 2.0, 2.0
+RATE, RATE_Z, LATE, COST = 41.0, 41.0, 0.95, 0.6
 NT = (((1,), (1,)), ((), ()))
 
 

time: 44.3 us -> 44.1 us (level)
  no operation moved by 1% of the time
where the time goes in v6:
time: 44.1 us; the launch traced here: 44 us
  Pallas kernels  43.3 us (98%)
  local copies, waits for them, and re-layouts  0.71 us (2%)
    pallas_call x1, Pallas kernels, body(): pl.pallas_call(functools.partial(kernel, copies), out_shape=jax.ShapeDtyp...  43.3 us

profile of v6, /device:TPU:1, one launch (start us, length us, event | category | flops | bytes accessed | tf_op | source)
XLA Modules:
  0.0 44.0 jit_solution(15031918384813803562)
XLA Ops:
  0.0 43.3 %shard_map.82 = bf16[128,1024]{1,0:T(8,128)(2,1)S(1)} custom-call(bf16[1024,1024]{1,0:T(8,128)(2,1)} %tokens.1, bf16[2,64,1024]{2,1,0:T(8,128)(2,1)} %bitcast.1, bf16[2,64]{1,0:T(2,128)(2,1)} %db_in.1, bf16[2,64,1024]{2,1,0:T(8,128)(2,1)} %up_in.1, bf16[2,1024]{1,0:T(2,128)(2,1)} %ub_in.1, bf16[4,1024]{1,0:T(4,128)(2,1)} %q_in.1, bf16[4,1024]{1,0:T(4,128)(2,1)} %k_in.1, ...), custom_call_target="tpu_custom_call" | custom-call | tf_op jit(solution)/shard_map/pallas_call | solution.py:399
  43.3 0.7 %copy.10 = bf16[128,1024]{1,0:T(8,128)(2,1)} copy(bf16[128,1024]{1,0:T(8,128)(2,1)S(1)} %shard_map.82) | data formatting | bytes 524288
